TPU v7x, 256 devices: a whole 4x4x8 slice. The times are simulated.
256 devices in a mesh: dp: 8 (over x, y_lo), tp: 32 (over y_hi, z, core).
Axes of the slice: x: 4, y: 4 (y_hi: 2, y_lo: 2; y = y_hi * 2 + y_lo), z: 8, core: 2. Of those that a mesh axis runs over, the one named last changes fastest.
Arguments:
- proj_in: bfloat16 [1, 32768, 8192], P(None, 'dp', 'tp'), may hold values from -6 to 6
- kv_grad: bfloat16 [1, 32768, 2048], P(None, ('dp', 'tp')), may hold values from -0.75 to 0.75
- normed: bfloat16 [1, 32768, 8192], P(None, ('dp', 'tp')), may hold values from -6 to 6
- norm_grad: bfloat16 [1, 32768, 8192], P(None, ('dp', 'tp')), may hold values from -0.6 to 0.6
- first_moment: float32 [1, 8192, 2048], P(None, 'tp', 'dp'), may hold values from -0.6 to 0.6
- second_moment: float32 [1, 8192, 2048], P(None, 'tp', 'dp'), may hold values from 0.002 to 0.02
Outputs:
- new_first: float32 [1, 8192, 2048], P(None, 'tp', 'dp')
- new_second: float32 [1, 8192, 2048], P(None, 'tp', 'dp')
- adam_step: float32 [1, 8192, 2048], P(None, 'tp', 'dp')
- gain_grad: float32 [1, 8192], replicated
All inputs are finite; a program needn't handle non-finite values.
Results may differ from a plain program's by a relative error of at most 0.0003.
Values may be sent and summed in bfloat16 or wider, within the bound.
A program may use at most 128 MiB of HBM per device.

v0:
```python
import functools

import jax
import jax.numpy as jnp
from jax import lax
from jax.sharding import Mesh
from jax.sharding import PartitionSpec as P

DP = ("dp_0", "dp_1")
DP_TP = ("dp_0", "dp_1", "tp_0", "tp_1", "tp_2")
TP = ("tp_0", "tp_1", "tp_2")


beta_one = 0.9
beta_two = 0.95
correct_one = 0.19
correct_two = 0.0975
epsilon = 1e-08


def over_axes(array, axes):
    return functools.reduce(lax.psum, axes, array)


def in_blocks(array, dim, size):
    lengths = array.shape
    pieces = array.reshape(*lengths[:dim], size, lengths[dim] // size, *lengths[dim + 1 :])
    return jnp.moveaxis(pieces, dim, 0)


def sent_and_summed(array, axis, dim):
    pieces = in_blocks(array, dim, lax.axis_size(axis))
    arrived = lax.all_to_all(pieces, axis, split_axis=0, concat_axis=0, tiled=True)
    return arrived.sum(axis=0)


def adam_update(mean_grad, first_old, second_old):
    new_first = beta_one * first_old + (1.0 - beta_one) * mean_grad
    new_second = beta_two * second_old + (1.0 - beta_two) * mean_grad * mean_grad
    update = new_first / correct_one / (jnp.sqrt(new_second / correct_two) + epsilon)
    return (new_first, new_second, update)


def row_adder(inputs, arrived):
    return lax.dot_general(
        inputs, arrived, (((0,), (0,)), ((), ())), preferred_element_type=jnp.float32
    )


def shards(proj_in, kv_grad, normed, norm_grad, first_moment, second_moment):
    replicas = lax.axis_size(DP)
    local_terms = jnp.sum(norm_grad.astype(jnp.float32) * normed.astype(jnp.float32), axis=1)
    gain_grad = over_axes(local_terms, DP_TP) / replicas
    inputs = proj_in[0]
    grad_rows = kv_grad[0]
    local_grad = row_adder(inputs, lax.all_gather(grad_rows, TP, axis=0, tiled=True))
    mean_grad = sent_and_summed(local_grad, DP, 1) / replicas
    new_first, new_second, update = adam_update(mean_grad, first_moment[0], second_moment[0])
    firsts = [new_first]
    seconds = [new_second]
    updates = [update]
    return (jnp.stack(firsts), jnp.stack(seconds), jnp.stack(updates), gain_grad)


def solution(mesh):
    finer = Mesh(mesh.devices.reshape(4, 2, 2, 8, 2), ("dp_0", "dp_1", "tp_0", "tp_1", "tp_2"))
    return jax.shard_map(
        shards,
        mesh=finer,
        in_specs=(
            P(None, DP, TP),
            P(None, DP_TP, None),
            P(None, DP_TP, None),
            P(None, DP_TP, None),
            P(None, TP, DP),
            P(None, TP, DP),
        ),
        out_specs=(P(None, TP, DP), P(None, TP, DP), P(None, TP, DP), P()),
        check_vma=False,
    )
```

profile of v0, /device:TPU:1, one launch (start us, length us, event | category | flops | bytes accessed | tf_op | source)
XLA Modules:
  0.0 229.3 jit_solution(13198261550055182338)
XLA Ops:
  7.2 0.0 copy-start
  7.2 0.0 all-gather.3.cloned.1.call-start
  7.2 0.7 all-gather.3.cloned.1.call-update
  7.9 2.8 %multiply_reduce_fusion = f32[8192]{0:T(1024)S(1)} fusion(bf16[1,128,8192]{2,1,0:T(8,128)(2,1)} %param.8, bf16[1,128,8192]{2,1,0:T(8,128)(2,1)} %param.9), kind=kLoop, calls=%fused_computation | loop fusion | flops 4186112 | bytes 4227072 | tf_op jit(solution)/shard_map/reduce_sum | solution.py:52
  10.7 14.3 %psum.35 = f32[1,8192]{1,0:T(1,128)S(1)} all-reduce(f32[1,8192]{1,0:T(1,128)S(1)} %bitcast.23), channel_id=1, replica_groups=mesh['dp_0'=4,'dp_1'=2,'tp_0'=2,'tp_1'=8,'tp_2'=2] {'dp_0'}, use_global_device_ids=true, to_apply=%region_2.0 | all-reduce | flops 8192 | bytes 65536 | tf_op jit(solution)/shard_map/psum | solution.py:22
  25.1 7.0 %psum.36 = f32[1,8192]{1,0:T(1,128)S(1)} all-reduce(f32[1,8192]{1,0:T(1,128)S(1)} %psum.35), channel_id=1, replica_groups=mesh['dp_0'=4,'dp_1'=2,'tp_0'=2,'tp_1'=8,'tp_2'=2] {'dp_1'}, use_global_device_ids=true, to_apply=%region_3.0 | all-reduce | flops 8192 | bytes 65536 | tf_op jit(solution)/shard_map/psum | solution.py:22
  32.1 9.2 %psum.37 = f32[1,8192]{1,0:T(1,128)S(1)} all-reduce(f32[1,8192]{1,0:T(1,128)S(1)} %psum.36), channel_id=1, replica_groups=mesh['dp_0'=4,'dp_1'=2,'tp_0'=2,'tp_1'=8,'tp_2'=2] {'tp_0'}, use_global_device_ids=true, to_apply=%region_4.0 | all-reduce | flops 8192 | bytes 65536 | tf_op jit(solution)/shard_map/psum | solution.py:22
  41.3 111.2 %all-gather.3.cloned.1.call-done = bf16[1,4096,2048]{2,1,0:T(8,128)(2,1)} async-done(((bf16[1,128,2048]{2,1,0:T(8,128)(2,1)}), bf16[1,4096,2048]{2,1,0:T(8,128)(2,1)}) %all-gather.3.cloned.1.call-update) | async-done | bytes 16777232 | tf_op jit(solution)/shard_map/all_gather | solution.py:56
  152.5 20.7 %copy.10 = bf16[2048,4096]{1,0:T(8,128)(2,1)} copy(bf16[2048,4096]{0,1:T(8,128)(2,1)} %bitcast.21) | data formatting | bytes 33554432 | tf_op jit(solution)/shard_map/dot_general | solution.py:45
  173.3 0.0 copy-done
  173.3 9.5 %fusion.2 = f32[8,256,256]{2,1,0:T(8,128)} fusion(bf16[8,256,4096]{2,1,0:T(8,128)(2,1)} %bitcast.22, bf16[1,4096,256]{2,1,0:T(8,128)(2,1)S(1)} %copy-done), kind=kOutput, calls=%fused_computation.3 | convolution fusion | flops 4294967296 | bytes 20971520 | tf_op jit(solution)/shard_map/dot_general | solution.py:45
  182.8 4.3 %all-to-all-start = ((f32[8,256,256]{2,1,0:T(8,128)}), f32[8,256,256]{2,1,0:T(8,128)}, u32[]{:S(2)}, u32[]{:S(2)}) async-start(f32[8,256,256]{2,1,0:T(8,128)} %fusion.2), calls=%async_computation | async-start | bytes 4194304 | tf_op jit(solution)/shard_map/all_to_all | solution.py:33
  187.1 0.0 copy-start.1
  187.2 0.0 copy-start.2
  187.2 24.0 %psum.38 = f32[1,8192]{1,0:T(1,128)S(1)} all-reduce(f32[1,8192]{1,0:T(1,128)S(1)} %psum.37), channel_id=1, replica_groups=mesh['dp_0'=4,'dp_1'=2,'tp_0'=2,'tp_1'=8,'tp_2'=2] {'tp_1'}, use_global_device_ids=true, to_apply=%region_5.0 | all-reduce | flops 8192 | bytes 65536 | tf_op jit(solution)/shard_map/psum | solution.py:22
  211.1 7.9 %psum.39 = f32[1,8192]{1,0:T(1,128)S(1)} all-reduce(f32[1,8192]{1,0:T(1,128)S(1)} %psum.38), channel_id=1, replica_groups=mesh['dp_0'=4,'dp_1'=2,'tp_0'=2,'tp_1'=8,'tp_2'=2] {'tp_2'}, use_global_device_ids=true, to_apply=%region_6.0 | all-reduce | flops 8192 | bytes 65536 | tf_op jit(solution)/shard_map/psum | solution.py:22
  219.1 0.6 broadcast_multiply_fusion
  219.7 0.0 all-to-all-done
  219.7 1.8 reduce_sum.20
  221.5 0.0 copy-done.1
  221.5 0.0 copy-done.2
  221.5 1.0 add_divide_fusion
Async XLA Ops:
  7.2 166.1 %copy-start = (bf16[1,4096,256]{2,1,0:T(8,128)(2,1)S(1)}, bf16[1,4096,256]{2,1,0:T(8,128)(2,1)}, u32[]{:S(2)}) copy-start(bf16[1,4096,256]{2,1,0:T(8,128)(2,1)} %param.6) | copy-start | bytes 6291460
  7.2 145.3 %all-gather.3.cloned.1.call-start = ((), (), s32[]{:S(2)}) async-start(), calls=%async_computation.1 | async-start | bytes 17301504 | tf_op jit(solution)/shard_map/all_gather | solution.py:56
  182.8 36.9 %all-to-all-start = ((f32[8,256,256]{2,1,0:T(8,128)}), f32[8,256,256]{2,1,0:T(8,128)}, u32[]{:S(2)}, u32[]{:S(2)}) async-start(f32[8,256,256]{2,1,0:T(8,128)} %fusion.2), calls=%async_computation | async-start | bytes 4194304 | tf_op jit(solution)/shard_map/all_to_all | solution.py:33
  187.1 34.3 %copy-start.1 = (f32[1,256,256]{2,1,0:T(8,128)S(1)}, f32[1,256,256]{2,1,0:T(8,128)}, u32[]{:S(2)}) copy-start(f32[1,256,256]{2,1,0:T(8,128)} %param.11) | copy-start | bytes 786436
  187.2 34.3 %copy-start.2 = (f32[1,256,256]{2,1,0:T(8,128)S(1)}, f32[1,256,256]{2,1,0:T(8,128)}, u32[]{:S(2)}) copy-start(f32[1,256,256]{2,1,0:T(8,128)} %param.10) | copy-start | bytes 786436
Sparse Core Ops, SparseCore 0:
  10.8 141.7 all-gather.2
where the time goes:
time: 230 us; the launch traced here: 229 us
  waiting for transfers between devices  112 us (49%)
  blocking collectives  62.4 us (27%)
  local copies, waits for them, and re-layouts  20.8 us (9%)
  between operations  14.1 us (6%)
  matrix products  9.54 us (4%)
  other arithmetic  6.19 us (3%)
  starting transfers between devices  4.38 us (2%)
    all_gather x1, waiting for transfers between devices, shards(): lax.all_gather(grad_rows, TP, axis=0, tiled=True)  111 us
    psum x5, blocking collectives, over_axes(): return functools.reduce(lax.psum, axes, array)  62.4 us
    dot_general x1, local copies, waits for them, and re-layouts, row_adder(): lax.dot_general(inputs, arrived, (((0,), (0,)), ((), ())), preferred_elem...  20.7 us
    dot_general x1, matrix products, row_adder(): lax.dot_general(inputs, arrived, (((0,), (0,)), ((), ())), preferred_elem...  9.54 us
  transfers between devices with their start and end apart: 2, of which 1 were waited for; matrix products, arithmetic and copies ran while one was open for 2% of the time, Pallas kernels for 0%

commit v1 on v0

v1 whole, which is shorter than its diff:
```python
import functools

import jax
import jax.numpy as jnp
from jax import lax
from jax.experimental import pallas as pl
from jax.experimental.pallas import tpu as pltpu
from jax.sharding import Mesh
from jax.sharding import PartitionSpec as P

X, YLO, YHI, Z, CORE = "dp_0", "dp_1", "tp_0", "tp_1", "tp_2"
DP = (X, YLO)
TP = (YHI, Z, CORE)
DP_TP = DP + TP
MESH = pl.DeviceIdType.MESH

beta_one = 0.9
beta_two = 0.95
correct_one = 0.19
correct_two = 0.0975
epsilon = 1e-08

ORDER = (
    ('XS',), ('S', 0), ('S', 1), ('XO', 0), ('XO', 1), ('XO', 2), ('XO', 3), ('GC',), ('E', 0, 1), ('R', 0), ('GX',),
    ('E', 1, 1), ('R', 1), ('GY',), ('E', 0, 2), ('R', 2), ('E', 1, 2), ('R', 3), ('E', 0, 3), ('XA', 0), ('S', 2),
    ('E', 1, 3), ('XA', 1), ('E', 0, 4), ('GZ',), ('M', 0, 0), ('E', 2, 1), ('XA', 2), ('E', 1, 4), ('GA',),
    ('M', 1, 0), ('XA', 3), ('X1', 0, 0), ('M', 0, 1), ('E', 2, 2), ('M', 1, 1), ('GO',), ('X1', 1, 0), ('S', 3),
    ('X2', 0, 0), ('E', 2, 3), ('X1', 0, 1), ('E', 3, 1), ('X1', 1, 1), ('E', 2, 4), ('M', 2, 0), ('X2', 1, 0),
    ('M', 2, 1), ('E', 3, 2), ('X2', 0, 1), ('X2', 1, 1), ('X1', 2, 0), ('Y1', 0, 0), ('Y1', 0, 1), ('E', 3, 3),
    ('X1', 2, 1), ('Y1', 1, 0), ('Y1', 1, 1), ('X2', 2, 0), ('E', 3, 4), ('Y2', 0), ('X2', 2, 1), ('M', 3, 0),
    ('M', 3, 1), ('Y2', 1), ('Y1', 2, 0), ('X1', 3, 0), ('Y1', 2, 1), ('X1', 3, 1), ('Y2', 2), ('X2', 3, 0),
    ('X2', 3, 1), ('Y1', 3, 0), ('Y1', 3, 1), ('Y2', 3),
)


def adam_update(mean_grad, first_old, second_old):
    new_first = beta_one * first_old + (1.0 - beta_one) * mean_grad
    new_second = beta_two * second_old + (1.0 - beta_two) * mean_grad * mean_grad
    update = new_first / correct_one / (jnp.sqrt(new_second / correct_two) + epsilon)
    return (new_first, new_second, update)


SCRATCH = dict(
    gbuf=pltpu.VMEM((4, 8, 2, 128, 512), jnp.bfloat16),
    xown=pltpu.VMEM((2048, 256), jnp.bfloat16),
    xoth=pltpu.VMEM((2, 4, 256, 256), jnp.bfloat16),
    relay=pltpu.VMEM((2, 4, 256, 256), jnp.bfloat16),
    xt=pltpu.VMEM((2, 256, 2048), jnp.bfloat16),
    part=pltpu.VMEM((4, 2, 4, 256, 128), jnp.float32),
    xfar=pltpu.VMEM((4, 2, 2, 128, 128), jnp.float32),
    xnear=pltpu.VMEM((4, 2, 2, 256, 128), jnp.float32),
    summed=pltpu.VMEM((4, 2, 256, 128), jnp.float32),
    yfar=pltpu.VMEM((4, 2, 128, 128), jnp.float32),
    ynear=pltpu.VMEM((4, 2, 256, 128), jnp.float32),
    nbuf=pltpu.VMEM((128, 8192), jnp.bfloat16),
    ngbuf=pltpu.VMEM((128, 8192), jnp.bfloat16),
    gain_c=pltpu.VMEM((2, 8, 8, 128), jnp.float32),
    gain_x=pltpu.VMEM((4, 8, 8, 128), jnp.float32),
    gain_y=pltpu.VMEM((4, 8, 8, 128), jnp.float32),
    gain_s=pltpu.VMEM((8, 8, 128), jnp.float32),
    gain_z=pltpu.VMEM((8, 8, 128), jnp.float32),
    gain_a=pltpu.VMEM((8, 8, 128), jnp.float32),
    load=pltpu.SemaphoreType.DMA((7,)),
    z_s=pltpu.SemaphoreType.DMA((4, 2, 4)),
    z_r=pltpu.SemaphoreType.DMA((4, 2, 4)),
    d_s=pltpu.SemaphoreType.DMA((4, 9)),
    d_r=pltpu.SemaphoreType.DMA((4, 9)),
    x1_s=pltpu.SemaphoreType.DMA((2, 4)),
    x1_r=pltpu.SemaphoreType.DMA((2, 4)),
    x2_s=pltpu.SemaphoreType.DMA((2, 4)),
    x2_r=pltpu.SemaphoreType.DMA((2, 4)),
    u_s=pltpu.SemaphoreType.DMA((4, 2, 6)),
    u_r=pltpu.SemaphoreType.DMA((4, 2, 6)),
    y_s=pltpu.SemaphoreType.DMA((4, 2, 2)),
    yf_r=pltpu.SemaphoreType.DMA((4, 2)),
    yn_r=pltpu.SemaphoreType.DMA((4, 2, 2)),
    g_s=pltpu.SemaphoreType.DMA((21,)),
    g_r=pltpu.SemaphoreType.DMA((21,)),
)


def exchange(x_hbm, g_hbm, n_hbm, ng_hbm, out_ref, gain_ref, *scratch):
    b = dict(zip(SCRATCH, scratch, strict=True))
    x, ylo, yhi = lax.axis_index(X), lax.axis_index(YLO), lax.axis_index(YHI)
    z, core = lax.axis_index(Z), lax.axis_index(CORE)
    y = yhi * 2 + ylo
    other = 1 - core

    def ring(value, size):
        return lax.rem(value + size, size)

    def at_x(step):
        return {X: ring(x + step, 4)}

    def at_y(step):
        there = ring(y + step, 4)
        return {YHI: there // 2, YLO: lax.rem(there, 2)}

    def at_z(step):
        return {Z: ring(z + step, 8)}

    sibling = {CORE: other}
    both = (1, -1)
    sent = []

    def copy(src, dst, send, recv, to):
        return pltpu.make_async_remote_copy(
            src_ref=src, dst_ref=dst, send_sem=send, recv_sem=recv, device_id=to, device_id_type=MESH
        )

    def start(*args):
        made = copy(*args)
        made.start()
        sent.append(made)

    loads = []
    for j in range(4):
        for k in range(4):
            first = k * 512 + (j % 2) * 256 + (j // 2) * 128
            loads.append(
                pltpu.make_async_copy(
                    g_hbm.at[:, pl.ds(first, 128)],
                    b["gbuf"].at[j, z, core, :, pl.ds(k * 128, 128)],
                    b["load"].at[j],
                )
            )
    own_rows = pl.multiple_of(yhi * 2048, 2048)
    away_rows = pl.multiple_of((1 - yhi) * 2048, 2048)
    load_x = pltpu.make_async_copy(x_hbm.at[pl.ds(own_rows, 2048), :], b["xown"], b["load"].at[4])
    load_n = pltpu.make_async_copy(n_hbm, b["nbuf"], b["load"].at[5])
    load_ng = pltpu.make_async_copy(ng_hbm, b["ngbuf"], b["load"].at[6])
    for one in loads:
        one.start()
    load_x.start()
    load_n.start()
    load_ng.start()

    barrier = pltpu.get_barrier_semaphore()
    greeted = [sibling]
    greeted += [at_x(k) for k in range(1, 4)] + [at_y(k) for k in range(1, 4)] + [at_z(k) for k in range(1, 8)]
    for peer in greeted:
        pl.semaphore_signal(barrier, inc=1, device_id=peer, device_id_type=MESH)
    pl.semaphore_wait(barrier, len(greeted))

    def z_copy(j, d, s, arriving):
        hops = s if arriving else s - 1
        source = ring(z - hops * both[d], 8)
        piece = b["gbuf"].at[j, source, core]
        if s == 4:
            piece = piece.at[pl.ds(64 * d, 64)]
        return piece, piece, b["z_s"].at[j, d, s - 1], b["z_r"].at[j, d, s - 1], at_z(both[d])

    def d_copy(j, d, s, half):
        source = z if s == 0 else ring(z - s * both[d], 8)
        piece = b["gbuf"].at[j, source, half]
        if s == 4:
            piece = piece.at[pl.ds(64 * d, 64)]
        slot = 0 if s == 0 else d * 4 + s
        return piece, piece, b["d_s"].at[j, slot], b["d_r"].at[j, slot], sibling

    def S(j):
        pltpu.make_async_copy(b["gbuf"].at[j, z, core], b["gbuf"].at[j, z, core], b["load"].at[j]).wait()
        for d in range(2):
            start(*z_copy(j, d, 1, False))
        start(*d_copy(j, 0, 0, core))

    def E(j, s):
        for d in range(2):
            copy(*z_copy(j, d, s, True)).wait_recv()
            if s < 4:
                start(*z_copy(j, d, s + 1, False))
            start(*d_copy(j, d, s, core))

    def relay_copy(d, m):
        rows = pl.multiple_of(away_rows + d * 1024 + m * 256, 256)
        return x_hbm.at[pl.ds(rows, 256), :], b["relay"].at[d, m], b["x1_s"].at[d, m], b["x1_r"].at[d, m], at_y(both[d])

    def onward_copy(d, m):
        return b["relay"].at[d, m], b["xoth"].at[d, m], b["x2_s"].at[d, m], b["x2_r"].at[d, m], at_y(both[d])

    def XS():
        for m in range(4):
            for d in range(2):
                start(*relay_copy(d, m))

    def R(m):
        for d in range(2):
            copy(*relay_copy(d, m)).wait_recv()
            start(*onward_copy(d, m))

    def XO(m):
        if m == 0:
            load_x.wait()
        for k in (2 * m, 2 * m + 1):
            b["xt"][0, :, k * 256 : (k + 1) * 256] = b["xown"][k * 256 : (k + 1) * 256, :].T

    def XA(m):
        for d in range(2):
            copy(*onward_copy(d, m)).wait_recv()
            k = d * 4 + m
            b["xt"][1, :, k * 256 : (k + 1) * 256] = b["xoth"][d, m].T

    def peers(at, me, count, buf, first, source=None):
        made = []
        for k in range(1, count):
            src = buf.at[me] if source is None else source.at[ring(me + k, count)]
            dst = buf.at[me]
            made.append((src, dst, b["g_s"].at[first + k - 1], b["g_r"].at[first + k - 1], at(k)))
        return made

    def arrived(me, count, buf, first, at):
        for k in range(1, count):
            piece = buf.at[ring(me - k, count)]
            copy(piece, piece, b["g_s"].at[first + k - 1], b["g_r"].at[first + k - 1], at(k)).wait_recv()

    def GC():
        load_n.wait()
        load_ng.wait()

        def block(i, carry):
            for k in range(8):
                lanes = pl.ds(pl.multiple_of(i * 1024 + k * 128, 128), 128)
                terms = b["nbuf"][:, lanes].astype(jnp.float32) * b["ngbuf"][:, lanes].astype(jnp.float32)
                b["gain_c"][core, i, k : k + 1, :] = jnp.sum(terms, axis=0, keepdims=True)
            return carry

        lax.fori_loop(0, 8, block, 0)
        mine = b["gain_c"].at[core]
        start(mine, mine, b["g_s"].at[0], b["g_r"].at[0], sibling)

    def GX():
        theirs = b["gain_c"].at[other]
        copy(theirs, theirs, b["g_s"].at[0], b["g_r"].at[0], sibling).wait_recv()
        b["gain_x"][x] = b["gain_c"][0] + b["gain_c"][1]
        for one in peers(at_x, x, 4, b["gain_x"], 1):
            start(*one)

    def GY():
        arrived(x, 4, b["gain_x"], 1, at_x)
        g = b["gain_x"]
        b["gain_y"][y] = (g[0] + g[1]) + (g[2] + g[3])
        for one in peers(at_y, y, 4, b["gain_y"], 4):
            start(*one)

    def GZ():
        arrived(y, 4, b["gain_y"], 4, at_y)
        g = b["gain_y"]
        b["gain_s"][...] = (g[0] + g[1]) + (g[2] + g[3])
        b["gain_z"][z] = b["gain_s"][z]
        for one in peers(at_z, z, 8, b["gain_z"], 7, b["gain_s"]):
            start(*one)

    def GA():
        arrived(z, 8, b["gain_z"], 7, at_z)
        total = b["gain_z"][0]
        for k in range(1, 8):
            total = total + b["gain_z"][k]
        b["gain_a"][z] = total
        for one in peers(at_z, z, 8, b["gain_a"], 14):
            start(*one)

    def GO():
        arrived(z, 8, b["gain_a"], 14, at_z)
        gain_ref[...] = b["gain_a"][...].reshape(64, 128)

    def M(j, o):
        if o == 0:
            copy(*d_copy(j, 0, 0, other)).wait_recv()
            for s in range(1, 5):
                for d in range(2):
                    copy(*d_copy(j, d, s, other)).wait_recv()
        for k in range(2):
            right = b["gbuf"][j, :, :, :, k * 256 : (k + 1) * 256].reshape(2048, 256)
            product = jnp.dot(b["xt"][o], right, preferred_element_type=jnp.float32)
            b["part"][j, o, 2 * k] = product[:, :128]
            b["part"][j, o, 2 * k + 1] = product[:, 128:]
        far = ring(x + 2, 4)
        for d in range(2):
            half = pl.ds(128 * d, 128)
            start(b["part"].at[j, o, far, half], b["xfar"].at[j, o, d], b["u_s"].at[j, o, d], b["u_r"].at[j, o, d], at_x(both[d]))
        for d in range(2):
            start(*near_copy(j, o, d, 1 - d, 2 + d))

    def near_copy(j, o, d, half, slot):
        rows = pl.ds(128 * half, 128)
        return (
            b["part"].at[j, o, ring(x + both[d], 4), rows],
            b["xnear"].at[j, o, d, rows],
            b["u_s"].at[j, o, slot],
            b["u_r"].at[j, o, slot],
            at_x(both[d]),
        )

    def X1(j, o):
        for d in range(2):
            piece = b["xfar"].at[j, o, d]
            copy(piece, piece, b["u_s"].at[j, o, d], b["u_r"].at[j, o, d], at_x(both[d])).wait_recv()
            there = ring(x + both[d], 4)
            rows = pl.ds(128 * d, 128)
            b["part"][j, o, there, rows] = b["part"][j, o, there, rows] + b["xfar"][j, o, d]
            start(*near_copy(j, o, d, d, 4 + d))

    def role(j, o):
        owns = ylo == j % 2
        ahead = lax.rem(ylo + o, 2)
        return owns, ahead

    def y_target(ahead):
        there = ring(y + 1 - 2 * ahead, 4)
        return {YHI: there // 2, YLO: lax.rem(there, 2)}

    def feature(o):
        return lax.rem(yhi + o, 2)

    def y_far(j, o, d):
        rows = pl.ds(128 * d, 128)
        return b["summed"].at[j, o, rows], b["yfar"].at[j, feature(o)], b["y_s"].at[j, o, d], b["yf_r"].at[j, feature(o)], at_y(both[d])

    def y_near(j, o, ahead, late):
        half = ahead if late else 1 - ahead
        rows = pl.ds(pl.multiple_of(128 * half, 128), 128)
        slot = 1 if late else 0
        return (
            b["summed"].at[j, o, rows],
            b["ynear"].at[j, ahead, rows],
            b["y_s"].at[j, o, slot],
            b["yn_r"].at[j, ahead, slot],
            y_target(ahead),
        )

    def X2(j, o):
        for d in range(2):
            for slot, half in ((2 + d, 1 - d), (4 + d, d)):
                piece = b["xnear"].at[j, o, d, pl.ds(128 * half, 128)]
                copy(piece, piece, b["u_s"].at[j, o, slot], b["u_r"].at[j, o, slot], at_x(both[d])).wait_recv()
        b["summed"][j, o] = b["part"][j, o, x] + (b["xnear"][j, o, 0] + b["xnear"][j, o, 1])
        owns, ahead = role(j, o)
        if o == 1:

            @pl.when(owns)
            def _():
                for d in range(2):
                    copy(*y_far(j, o, d)).start()

        @pl.when(jnp.logical_not(owns))
        def _():
            copy(*y_near(j, o, ahead, False)).start()

    def Y1(j, o):
        owns, ahead = role(j, o)

        @pl.when(jnp.logical_not(owns))
        def _():
            piece = b["yfar"].at[j, feature(o)]
            copy(piece, piece, b["y_s"].at[j, o, 1], b["yf_r"].at[j, feature(o)], y_target(ahead)).wait_recv()
            rows = pl.ds(pl.multiple_of(128 * ahead, 128), 128)
            b["summed"][j, o, rows] = b["summed"][j, o, rows] + b["yfar"][j, feature(o)]
            copy(*y_near(j, o, ahead, True)).start()

    def Y2(j):
        owns, _ = role(j, 0)

        @pl.when(owns)
        def _():
            for side in range(2):
                for slot in range(2):
                    half = side if slot else 1 - side
                    piece = b["ynear"].at[j, side, pl.ds(128 * half, 128)]
                    copy(piece, piece, b["y_s"].at[j, 0, 0], b["yn_r"].at[j, side, slot], at_y(1)).wait_recv()
            total = b["summed"][j, 0] + (b["ynear"][j, 0] + b["ynear"][j, 1])
            first = (j // 2) * 128
            out_ref[:, first : first + 128] = total * 0.125

    steps = dict(S=S, E=E, XS=XS, R=R, XO=XO, XA=XA, GC=GC, GX=GX, GY=GY, GZ=GZ, GA=GA, GO=GO, M=M, X1=X1, X2=X2, Y1=Y1, Y2=Y2)
    for name, *which in ORDER:
        steps[name](*which)

    for one in sent:
        one.wait_send()
    for j in range(4):
        for o in range(2):
            owns, ahead = role(j, o)
            if o == 1:

                @pl.when(owns)
                def _():
                    for d in range(2):
                        copy(*y_far(j, o, d)).wait_send()

            @pl.when(jnp.logical_not(owns))
            def _():
                copy(*y_near(j, o, ahead, False)).wait_send()
                copy(*y_near(j, o, ahead, True)).wait_send()


def shards(proj_in, kv_grad, normed, norm_grad, first_moment, second_moment):
    mean_grad, gain = pl.pallas_call(
        exchange,
        out_shape=(jax.ShapeDtypeStruct((256, 256), jnp.float32), jax.ShapeDtypeStruct((64, 128), jnp.float32)),
        in_specs=[pl.BlockSpec(memory_space=pl.ANY)] * 4,
        out_specs=(pl.BlockSpec(memory_space=pltpu.VMEM), pl.BlockSpec(memory_space=pltpu.VMEM)),
        scratch_shapes=list(SCRATCH.values()),
        compiler_params=pltpu.CompilerParams(
            collective_id=0, has_side_effects=True, vmem_limit_bytes=60 * 1024 * 1024
        ),
        name="exchange",
    )(proj_in[0], kv_grad[0], normed[0], norm_grad[0])
    new_first, new_second, update = adam_update(mean_grad, first_moment[0], second_moment[0])
    gain_grad = (gain * 0.125).reshape(1, 8192)
    return (new_first[None], new_second[None], update[None], gain_grad)


def solution(mesh):
    finer = Mesh(mesh.devices.reshape(4, 2, 2, 8, 2), DP_TP)
    return jax.shard_map(
        shards,
        mesh=finer,
        in_specs=(
            P(None, DP, TP),
            P(None, DP_TP, None),
            P(None, DP_TP, None),
            P(None, DP_TP, None),
            P(None, TP, DP),
            P(None, TP, DP),
        ),
        out_specs=(P(None, TP, DP), P(None, TP, DP), P(None, TP, DP), P()),
        check_vma=False,
    )
```

time: 230 us -> 87.9 us (0.38)
  the two profiles are of different devices: /device:TPU:1 before, /device:TPU:8 now
where the time goes in v1:
time: 87.9 us; the launch traced here: 87.7 us
  Pallas kernels  83.8 us (95%)
  other arithmetic  3.29 us (4%)
    pallas_call x1, Pallas kernels, shards(): pl.pallas_call(exchange, out_shape=(jax.ShapeDtypeStruct((256, 256), jnp....  83.8 us
    broadcast_in_dim x1, other arithmetic, shards(): return (new_first[None], new_second[None], update[None], gain_grad)  1.91 us

profile of v1, /device:TPU:8, one launch (start us, length us, event | category | flops | bytes accessed | tf_op | source)
XLA Modules:
  0.0 87.7 jit_solution(17302667137724153012)
XLA Ops:
  0.6 0.0 copy-start
  0.6 0.0 copy-start.1
  0.7 83.8 %exchange.1 = (f32[256,256]{1,0:T(8,128)}, f32[64,128]{1,0:T(8,128)}) custom-call(bf16[4096,256]{1,0:T(8,128)(2,1)} %bitcast.23, bf16[128,2048]{1,0:T(8,128)(2,1)} %bitcast.26, bf16[128,8192]{1,0:T(8,128)(2,1)} %bitcast.24, bf16[128,8192]{1,0:T(8,128)(2,1)} %bitcast.25), custom_call_target="tpu_custom_call" | custom-call | tf_op jit(solution)/shard_map/exchange/pallas_call | solution.py:397
  84.4 1.4 %broadcast_multiply_fusion = f32[64,128]{1,0:T(8,128)} fusion(f32[64,128]{1,0:T(8,128)} %get-tuple-element.7), kind=kLoop, calls=%fused_computation.6 | loop fusion | flops 8192 | bytes 65536 | tf_op jit(solution)/shard_map/mul | solution.py:409
  85.8 0.0 copy-done
  85.8 0.0 copy-done.1
  85.8 1.9 %divide_bitcast_fusion = (f32[1,256,256]{2,1,0:T(8,128)}, f32[1,256,256]{2,1,0:T(8,128)}, f32[1,256,256]{2,1,0:T(8,128)}) fusion(f32[256,256]{1,0:T(8,128)} %get-tuple-element.6, f32[1,256,256]{2,1,0:T(8,128)S(1)} %copy-done, f32[1,256,256]{2,1,0:T(8,128)S(1)} %copy-done.1), kind=kLoop, calls=%fused_computation.3 | loop fusion | flops 720896 | bytes 1572864 | tf_op jit(solution)/shard_map/broadcast_in_dim | solution.py:410
Async XLA Ops:
  0.6 85.2 %copy-start = (f32[1,256,256]{2,1,0:T(8,128)S(1)}, f32[1,256,256]{2,1,0:T(8,128)}, u32[]{:S(2)}) copy-start(f32[1,256,256]{2,1,0:T(8,128)} %param.10) | copy-start | bytes 786436
  0.6 85.2 %copy-start.1 = (f32[1,256,256]{2,1,0:T(8,128)S(1)}, f32[1,256,256]{2,1,0:T(8,128)}, u32[]{:S(2)}) copy-start(f32[1,256,256]{2,1,0:T(8,128)} %param.11) | copy-start | bytes 786436

commit v2 on v1

v2 whole, which is shorter than its diff:
```python
import functools

import jax
import jax.numpy as jnp
from jax import lax
from jax.experimental import pallas as pl
from jax.experimental.pallas import tpu as pltpu
from jax.sharding import Mesh
from jax.sharding import PartitionSpec as P

X, YLO, YHI, Z, CORE = "dp_0", "dp_1", "tp_0", "tp_1", "tp_2"
DP = (X, YLO)
TP = (YHI, Z, CORE)
DP_TP = DP + TP
MESH = pl.DeviceIdType.MESH

beta_one = 0.9
beta_two = 0.95
correct_one = 0.19
correct_two = 0.0975
epsilon = 1e-08

VMEM_LIMIT = 60 * 1024 * 1024

ORDER = (
    ('S', 0), ('XS',), ('S', 1), ('S', 2), ('E', 0, 1), ('E', 1, 1), ('E', 2, 1), ('S', 3), ('E', 1, 2), ('GS',),
    ('R', 0), ('E', 0, 2), ('S', 4), ('E', 2, 2), ('R', 3), ('E', 0, 3), ('E', 1, 3), ('E', 4, 1), ('R', 1),
    ('E', 2, 3), ('E', 3, 1), ('S', 5), ('GX',), ('E', 0, 4), ('E', 1, 4), ('R', 2), ('M', 0, 0), ('M', 1, 0),
    ('E', 4, 2), ('XA', 3), ('E', 2, 4), ('S', 6), ('XA', 0), ('XA', 1), ('M', 2, 0), ('E', 3, 2), ('E', 5, 1),
    ('X1', 0, 0), ('X1', 1, 0), ('XA', 2), ('M', 2, 1), ('M', 0, 1), ('M', 1, 1), ('E', 4, 3), ('S', 7), ('E', 3, 3),
    ('E', 6, 1), ('E', 5, 2), ('X1', 2, 1), ('X1', 0, 1), ('E', 4, 4), ('X1', 2, 0), ('M', 4, 0), ('E', 3, 4),
    ('M', 4, 1), ('E', 7, 1), ('GY',), ('E', 6, 2), ('M', 3, 0), ('X2', 2, 1), ('M', 3, 1), ('E', 5, 3), ('X1', 4, 1),
    ('X1', 4, 0), ('E', 7, 2), ('X1', 1, 1), ('E', 6, 3), ('E', 5, 4), ('X1', 3, 0), ('X1', 3, 1), ('GZ',),
    ('X2', 0, 0), ('E', 7, 3), ('M', 5, 0), ('X2', 1, 0), ('E', 6, 4), ('X2', 0, 1), ('M', 5, 1), ('X2', 4, 0),
    ('X2', 3, 0), ('X2', 4, 1), ('M', 6, 0), ('E', 7, 4), ('X2', 3, 1), ('M', 7, 0), ('X2', 2, 0), ('M', 7, 1),
    ('X2', 1, 1), ('Y1', 4, 1), ('M', 6, 1), ('Y1', 0, 1), ('Y1', 1, 0), ('Y1', 3, 1), ('X1', 5, 1), ('Y1', 1, 1),
    ('Y1', 4, 0), ('X1', 7, 1), ('X1', 6, 1), ('Y1', 2, 0), ('Y1', 2, 1), ('Y1', 0, 0), ('X1', 5, 0), ('Y1', 3, 0),
    ('X1', 7, 0), ('X2', 5, 1), ('GA',), ('X2', 7, 1), ('X1', 6, 0), ('X2', 6, 1), ('X2', 5, 0), ('X2', 7, 0),
    ('Y1', 7, 0), ('Y2', 1), ('Y2', 3), ('Y1', 5, 0), ('X2', 6, 0), ('Y1', 6, 1), ('Y1', 6, 0), ('Y1', 5, 1),
    ('Y2', 4), ('Y2', 5), ('Y2', 0), ('Y2', 2), ('Y1', 7, 1), ('GO',), ('Y2', 7), ('Y2', 6),
)


SCRATCH = dict(
    raw=pltpu.VMEM((128, 2048), jnp.bfloat16),
    gbuf=pltpu.VMEM((8, 8, 2, 128, 256), jnp.bfloat16),
    xown=pltpu.VMEM((2048, 256), jnp.bfloat16),
    xoth=pltpu.VMEM((2, 4, 256, 256), jnp.bfloat16),
    relay=pltpu.VMEM((2, 4, 256, 256), jnp.bfloat16),
    xt=pltpu.VMEM((2, 256, 2048), jnp.bfloat16),
    part=pltpu.VMEM((8, 2, 4, 128, 128), jnp.float32),
    xfar=pltpu.VMEM((8, 2, 2, 64, 128), jnp.float32),
    xnear=pltpu.VMEM((8, 2, 2, 128, 128), jnp.float32),
    summed=pltpu.VMEM((8, 2, 128, 128), jnp.float32),
    yfar=pltpu.VMEM((8, 2, 64, 128), jnp.float32),
    ynear=pltpu.VMEM((8, 2, 128, 128), jnp.float32),
    nbuf=pltpu.VMEM((128, 8192), jnp.bfloat16),
    ngbuf=pltpu.VMEM((128, 8192), jnp.bfloat16),
    gain_c=pltpu.VMEM((2, 8, 8, 128), jnp.float32),
    gain_x=pltpu.VMEM((4, 8, 8, 128), jnp.float32),
    gain_y=pltpu.VMEM((4, 8, 8, 128), jnp.float32),
    gain_s=pltpu.VMEM((8, 8, 128), jnp.float32),
    gain_z=pltpu.VMEM((8, 8, 128), jnp.float32),
    gain_a=pltpu.VMEM((8, 8, 128), jnp.float32),
    load=pltpu.SemaphoreType.DMA((4,)),
    z_s=pltpu.SemaphoreType.DMA((8,)),
    z_r=pltpu.SemaphoreType.DMA((8, 4)),
    d_s=pltpu.SemaphoreType.DMA((8,)),
    d_r=pltpu.SemaphoreType.DMA((8,)),
    x1_s=pltpu.SemaphoreType.DMA,
    x1_r=pltpu.SemaphoreType.DMA((4,)),
    x2_s=pltpu.SemaphoreType.DMA,
    x2_r=pltpu.SemaphoreType.DMA((4,)),
    u_s=pltpu.SemaphoreType.DMA((8, 2)),
    far_r=pltpu.SemaphoreType.DMA((8, 2)),
    near_r=pltpu.SemaphoreType.DMA((8, 2)),
    y_s=pltpu.SemaphoreType.DMA((8, 2)),
    yf_r=pltpu.SemaphoreType.DMA((8, 2)),
    yn_r=pltpu.SemaphoreType.DMA((8,)),
    g_s=pltpu.SemaphoreType.DMA((5,)),
    g_r=pltpu.SemaphoreType.DMA((5,)),
)


def exchange(x_hbm, g_hbm, n_hbm, ng_hbm, out_ref, gain_ref, *scratch):
    b = dict(zip(SCRATCH, scratch, strict=True))
    x, ylo, yhi = lax.axis_index(X), lax.axis_index(YLO), lax.axis_index(YHI)
    z, core = lax.axis_index(Z), lax.axis_index(CORE)
    y = yhi * 2 + ylo
    other = 1 - core

    def ring(value, size):
        return lax.rem(value + size, size)

    def at_x(step):
        return {X: ring(x + step, 4)}

    def at_y(step):
        there = ring(y + step, 4)
        return {YHI: there // 2, YLO: lax.rem(there, 2)}

    def at_z(step):
        return {Z: ring(z + step, 8)}

    sibling = {CORE: other}
    both = (1, -1)

    def copy(src, dst, send, recv, to):
        return pltpu.make_async_remote_copy(
            src_ref=src, dst_ref=dst, send_sem=send, recv_sem=recv, device_id=to, device_id_type=MESH
        )

    def start(*args):
        copy(*args).start()

    def landed(ref, sem):
        pltpu.make_async_copy(ref, ref, sem).wait()

    own_rows = pl.multiple_of(yhi * 2048, 2048)
    away_rows = pl.multiple_of((1 - yhi) * 2048, 2048)
    load_g = pltpu.make_async_copy(g_hbm, b["raw"], b["load"].at[0])
    load_x = pltpu.make_async_copy(x_hbm.at[pl.ds(own_rows, 2048), :], b["xown"], b["load"].at[1])
    load_n = pltpu.make_async_copy(n_hbm, b["nbuf"], b["load"].at[2])
    load_ng = pltpu.make_async_copy(ng_hbm, b["ngbuf"], b["load"].at[3])
    for one in (load_g, load_x, load_n, load_ng):
        one.start()

    barrier = pltpu.get_barrier_semaphore()
    greeted = [sibling, at_z(1), at_z(-1)] + [at_y(k) for k in range(1, 4)] + [at_x(k) for k in range(1, 4)]
    for peer in greeted:
        pl.semaphore_signal(barrier, inc=1, device_id=peer, device_id_type=MESH)

    load_g.wait()
    for low in range(2):
        for pair in range(2):
            blocks = []
            for k in range(4):
                first = k * 512 + low * 256 + pair * 128
                blocks.append(b["raw"][:, first : first + 128])
            for side in range(2):
                lanes = slice(64 * side, 64 * side + 64)
                j = (pair * 2 + side) * 2 + low
                b["gbuf"][j, z, core] = jnp.concatenate([block[:, lanes] for block in blocks], axis=1)
    load_x.wait()
    for k in range(8):
        b["xt"][0, :, k * 256 : (k + 1) * 256] = b["xown"][k * 256 : (k + 1) * 256, :].T
    load_n.wait()
    load_ng.wait()

    def block_sum(i, carry):
        for k in range(8):
            lanes = pl.ds(pl.multiple_of(i * 1024 + k * 128, 128), 128)
            terms = b["nbuf"][:, lanes].astype(jnp.float32) * b["ngbuf"][:, lanes].astype(jnp.float32)
            b["gain_c"][core, i, k : k + 1, :] = jnp.sum(terms, axis=0, keepdims=True)
        return carry

    lax.fori_loop(0, 8, block_sum, 0)
    pl.semaphore_wait(barrier, len(greeted))

    def z_send(j, d, s):
        piece = b["gbuf"].at[j, ring(z - (s - 1) * both[d], 8), core]
        if s == 4:
            piece = piece.at[pl.ds(64 * d, 64)]
        start(piece, piece, b["z_s"].at[j], b["z_r"].at[j, s - 1], at_z(both[d]))

    def d_send(j, d, s):
        piece = b["gbuf"].at[j, ring(z - s * both[d], 8), core]
        if s == 4:
            piece = piece.at[pl.ds(64 * d, 64)]
        start(piece, piece, b["d_s"].at[j], b["d_r"].at[j], sibling)

    def S(j):
        for d in range(2):
            z_send(j, d, 1)
        d_send(j, 0, 0)

    def E(j, s):
        landed(b["gbuf"].at[j, pl.ds(0, 2 if s < 4 else 1), core], b["z_r"].at[j, s - 1])
        for d in range(2):
            if s < 4:
                z_send(j, d, s + 1)
            d_send(j, d, s)

    def relay_copy(d, m):
        rows = pl.multiple_of(away_rows + d * 1024 + m * 256, 256)
        return x_hbm.at[pl.ds(rows, 256), :], b["relay"].at[d, m], b["x1_s"], b["x1_r"].at[m], at_y(both[d])

    def onward_copy(d, m):
        return b["relay"].at[d, m], b["xoth"].at[d, m], b["x2_s"], b["x2_r"].at[m], at_y(both[d])

    def XS():
        for m in range(4):
            for d in range(2):
                start(*relay_copy(d, m))

    def R(m):
        landed(b["relay"].at[:, m], b["x1_r"].at[m])
        for d in range(2):
            start(*onward_copy(d, m))

    def XA(m):
        landed(b["xoth"].at[:, m], b["x2_r"].at[m])
        for d in range(2):
            k = d * 4 + m
            b["xt"][1, :, k * 256 : (k + 1) * 256] = b["xoth"][d, m].T

    def spread(at, me, count, buf, sem, source=None):
        for k in range(1, count):
            src = buf.at[me] if source is None else source.at[ring(me + k, count)]
            start(src, buf.at[me], b["g_s"].at[sem], b["g_r"].at[sem], at(k))

    def arrived(count, buf, sem):
        landed(buf.at[pl.ds(0, count - 1)], b["g_r"].at[sem])

    def GS():
        mine = b["gain_c"].at[core]
        start(mine, mine, b["g_s"].at[0], b["g_r"].at[0], sibling)

    def GX():
        landed(b["gain_c"].at[0], b["g_r"].at[0])
        b["gain_x"][x] = b["gain_c"][0] + b["gain_c"][1]
        spread(at_x, x, 4, b["gain_x"], 1)

    def GY():
        arrived(4, b["gain_x"], 1)
        g = b["gain_x"]
        b["gain_y"][y] = (g[0] + g[1]) + (g[2] + g[3])
        spread(at_y, y, 4, b["gain_y"], 2)

    def GZ():
        arrived(4, b["gain_y"], 2)
        g = b["gain_y"]
        b["gain_s"][...] = (g[0] + g[1]) + (g[2] + g[3])
        b["gain_z"][z] = b["gain_s"][z]
        spread(at_z, z, 8, b["gain_z"], 3, b["gain_s"])

    def GA():
        arrived(8, b["gain_z"], 3)
        total = b["gain_z"][0]
        for k in range(1, 8):
            total = total + b["gain_z"][k]
        b["gain_a"][z] = total
        spread(at_z, z, 8, b["gain_a"], 4)

    def GO():
        arrived(8, b["gain_a"], 4)
        gain_ref[...] = b["gain_a"][...]

    def M(j, o):
        if o == 0:
            landed(b["gbuf"].at[j, :, other], b["d_r"].at[j])
        low = lax.broadcasted_iota(jnp.int32, (128, 128), 1) < 64
        packed = []
        for h in range(2):
            product = jnp.dot(
                b["xt"][o, :, h * 1024 : (h + 1) * 1024],
                b["gbuf"][j, 4 * h : 4 * h + 4].reshape(1024, 256),
                preferred_element_type=jnp.float32,
            )
            for k in range(2):
                lanes = slice(128 * k, 128 * k + 128)
                upper, lower = product[:128, lanes], product[128:, lanes]
                packed.append(jnp.where(low, upper, pltpu.roll(lower, 64, 1)))
                packed.append(jnp.where(low, pltpu.roll(upper, 64, 1), lower))
        for k in range(4):
            b["part"][j, o, k] = packed[k] + packed[4 + k]
        far = ring(x + 2, 4)
        for d in range(2):
            half = pl.ds(64 * d, 64)
            start(b["part"].at[j, o, far, half], b["xfar"].at[j, o, d], b["u_s"].at[j, o], b["far_r"].at[j, o], at_x(both[d]))
        for d in range(2):
            near_send(j, o, d, 1 - d)

    def near_send(j, o, d, half):
        rows = pl.ds(64 * half, 64)
        start(
            b["part"].at[j, o, ring(x + both[d], 4), rows],
            b["xnear"].at[j, o, d, rows],
            b["u_s"].at[j, o],
            b["near_r"].at[j, o],
            at_x(both[d]),
        )

    def X1(j, o):
        landed(b["xfar"].at[j, o], b["far_r"].at[j, o])
        for d in range(2):
            there = ring(x + both[d], 4)
            rows = pl.ds(64 * d, 64)
            b["part"][j, o, there, rows] = b["part"][j, o, there, rows] + b["xfar"][j, o, d]
            near_send(j, o, d, d)

    def role(j, o):
        owns = ylo == j % 2
        ahead = lax.rem(ylo + o, 2)
        return owns, ahead

    def y_target(ahead):
        there = ring(y + 1 - 2 * ahead, 4)
        return {YHI: there // 2, YLO: lax.rem(there, 2)}

    def feature(o):
        return lax.rem(yhi + o, 2)

    def y_far(j, o, d):
        rows = pl.ds(64 * d, 64)
        return b["summed"].at[j, o, rows], b["yfar"].at[j, feature(o)], b["y_s"].at[j, o], b["yf_r"].at[j, feature(o)], at_y(both[d])

    def y_near(j, o, ahead, late):
        half = ahead if late else 1 - ahead
        rows = pl.ds(pl.multiple_of(64 * half, 64), 64)
        return (
            b["summed"].at[j, o, rows],
            b["ynear"].at[j, ahead, rows],
            b["y_s"].at[j, o],
            b["yn_r"].at[j],
            y_target(ahead),
        )

    def X2(j, o):
        landed(b["xnear"].at[j, o], b["near_r"].at[j, o])
        b["summed"][j, o] = b["part"][j, o, x] + (b["xnear"][j, o, 0] + b["xnear"][j, o, 1])
        owns, ahead = role(j, o)
        if o == 1:

            @pl.when(owns)
            def _():
                for d in range(2):
                    copy(*y_far(j, o, d)).start()

        @pl.when(jnp.logical_not(owns))
        def _():
            copy(*y_near(j, o, ahead, False)).start()

    def Y1(j, o):
        owns, ahead = role(j, o)

        @pl.when(jnp.logical_not(owns))
        def _():
            landed(b["yfar"].at[j, feature(o)], b["yf_r"].at[j, feature(o)])
            rows = pl.ds(pl.multiple_of(64 * ahead, 64), 64)
            b["summed"][j, o, rows] = b["summed"][j, o, rows] + b["yfar"][j, feature(o)]
            copy(*y_near(j, o, ahead, True)).start()

    def Y2(j):
        owns, _ = role(j, 0)

        @pl.when(owns)
        def _():
            landed(b["ynear"].at[j], b["yn_r"].at[j])
            total = b["summed"][j, 0] + (b["ynear"][j, 0] + b["ynear"][j, 1])
            total = total * 0.125
            lanes = slice((j // 2) * 64, (j // 2) * 64 + 64)
            out_ref[:128, lanes] = total[:, :64]
            out_ref[128:, lanes] = total[:, 64:]

    steps = dict(S=S, E=E, XS=XS, R=R, XA=XA, GS=GS, GX=GX, GY=GY, GZ=GZ, GA=GA, GO=GO, M=M, X1=X1, X2=X2, Y1=Y1, Y2=Y2)
    for name, *which in ORDER:
        steps[name](*which)

    landed(x_hbm.at[pl.ds(0, 2048), :], b["x1_s"])
    landed(b["xoth"], b["x2_s"])
    for sem, piece in enumerate((b["gain_c"].at[0], b["gain_x"].at[pl.ds(0, 3)], b["gain_y"].at[pl.ds(0, 3)])):
        landed(piece, b["g_s"].at[sem])
    for sem in (3, 4):
        landed(b["gain_a"].at[pl.ds(0, 7)], b["g_s"].at[sem])
    for j in range(8):
        landed(b["gbuf"].at[j, pl.ds(0, 7), 0], b["z_s"].at[j])
        landed(b["gbuf"].at[j, :, 0], b["d_s"].at[j])
        for o in range(2):
            landed(b["part"].at[j, o, pl.ds(0, 3)], b["u_s"].at[j, o])
            owns, _ = role(j, o)
            if o == 1:
                landed(b["summed"].at[j, o], b["y_s"].at[j, o])
            else:

                @pl.when(jnp.logical_not(owns))
                def _():
                    landed(b["summed"].at[j, o], b["y_s"].at[j, o])


def finish(grad_ref, gain_ref, first_ref, second_ref, new_first_ref, new_second_ref, update_ref, gain_grad_ref):
    grad = grad_ref[...]
    new_first = beta_one * first_ref[...] + (1.0 - beta_one) * grad
    new_second = beta_two * second_ref[...] + (1.0 - beta_two) * grad * grad
    new_first_ref[...] = new_first
    new_second_ref[...] = new_second
    update_ref[...] = new_first / correct_one / (jnp.sqrt(new_second / correct_two) + epsilon)
    for i in range(8):
        for k in range(8):
            first = (i * 8 + k) * 128
            gain_grad_ref[0:1, first : first + 128] = gain_ref[i, k : k + 1, :] * 0.125


def shards(proj_in, kv_grad, normed, norm_grad, first_moment, second_moment):
    vmem = pl.BlockSpec(memory_space=pltpu.VMEM)
    mean_grad, gain = pl.pallas_call(
        exchange,
        out_shape=(jax.ShapeDtypeStruct((256, 256), jnp.float32), jax.ShapeDtypeStruct((8, 8, 128), jnp.float32)),
        in_specs=[pl.BlockSpec(memory_space=pltpu.HBM)] * 4,
        out_specs=(vmem, vmem),
        scratch_shapes=list(SCRATCH.values()),
        compiler_params=pltpu.CompilerParams(
            collective_id=0, has_side_effects=True, vmem_limit_bytes=VMEM_LIMIT
        ),
        name="exchange",
    )(proj_in[0], kv_grad[0], normed[0], norm_grad[0])
    block = jax.ShapeDtypeStruct((256, 256), jnp.float32)
    new_first, new_second, update, gain_grad = pl.pallas_call(
        finish,
        out_shape=(block, block, block, jax.ShapeDtypeStruct((1, 8192), jnp.float32)),
        in_specs=[vmem] * 4,
        out_specs=(vmem,) * 4,
        name="finish",
    )(mean_grad, gain, first_moment[0], second_moment[0])
    return (new_first[None], new_second[None], update[None], gain_grad)


def solution(mesh):
    finer = Mesh(mesh.devices.reshape(4, 2, 2, 8, 2), DP_TP)
    return jax.shard_map(
        shards,
        mesh=finer,
        in_specs=(
            P(None, DP, TP),
            P(None, DP_TP, None),
            P(None, DP_TP, None),
            P(None, DP_TP, None),
            P(None, TP, DP),
            P(None, TP, DP),
        ),
        out_specs=(P(None, TP, DP), P(None, TP, DP), P(None, TP, DP), P()),
        check_vma=False,
    )
```

time: 87.9 us -> 80 us (0.910)
  the two profiles are of different devices: /device:TPU:8 before, /device:TPU:1 now
where the time goes in v2:
time: 80 us; the launch traced here: 79.9 us
  Pallas kernels  79.3 us (99%)
    pallas_call x1, Pallas kernels, shards(): pl.pallas_call(exchange, out_shape=(jax.ShapeDtypeStruct((256, 256), jnp....  77.2 us
    pallas_call x1, Pallas kernels, shards(): pl.pallas_call(finish, out_shape=(block, block, block, jax.ShapeDtypeStru...  2.11 us

profile of v2, /device:TPU:1, one launch (start us, length us, event | category | flops | bytes accessed | tf_op | source)
XLA Modules:
  0.0 79.9 jit_solution(12275893314732186335)
XLA Ops:
  0.6 77.2 %exchange.1 = (f32[256,256]{1,0:T(8,128)}, f32[8,8,128]{2,1,0:T(8,128)}) custom-call(bf16[4096,256]{1,0:T(8,128)(2,1)} %bitcast.9, bf16[128,2048]{1,0:T(8,128)(2,1)} %bitcast.12, bf16[128,8192]{1,0:T(8,128)(2,1)} %bitcast.10, bf16[128,8192]{1,0:T(8,128)(2,1)} %bitcast.11), custom_call_target="tpu_custom_call" | custom-call | tf_op jit(solution)/shard_map/exchange/pallas_call | solution.py:396
  77.8 2.1 %finish.1 = (f32[256,256]{1,0:T(8,128)}, f32[256,256]{1,0:T(8,128)}, f32[256,256]{1,0:T(8,128)}, f32[1,8192]{1,0:T(1,128)}) custom-call(f32[256,256]{1,0:T(8,128)} %get-tuple-element.10.grad_ref, f32[8,8,128]{2,1,0:T(8,128)} %get-tuple-element.11.gain_ref, f32[256,256]{1,0:T(8,128)} %bitcast.13, f32[256,256]{1,0:T(8,128)} %bitcast.14), custom_call_target="tpu_custom_call" | custom-call | tf_op jit(solution)/shard_map/finish/pallas_call | solution.py:408

commit v3 on v2

--- a/solution.py
+++ b/solution.py
@@ -22,22 +22,25 @@
 
 VMEM_LIMIT = 60 * 1024 * 1024
 
+YFIRST = (6,)
 ORDER = (
-    ('S', 0), ('XS',), ('S', 1), ('S', 2), ('E', 0, 1), ('E', 1, 1), ('E', 2, 1), ('S', 3), ('E', 1, 2), ('GS',),
-    ('R', 0), ('E', 0, 2), ('S', 4), ('E', 2, 2), ('R', 3), ('E', 0, 3), ('E', 1, 3), ('E', 4, 1), ('R', 1),
-    ('E', 2, 3), ('E', 3, 1), ('S', 5), ('GX',), ('E', 0, 4), ('E', 1, 4), ('R', 2), ('M', 0, 0), ('M', 1, 0),
-    ('E', 4, 2), ('XA', 3), ('E', 2, 4), ('S', 6), ('XA', 0), ('XA', 1), ('M', 2, 0), ('E', 3, 2), ('E', 5, 1),
-    ('X1', 0, 0), ('X1', 1, 0), ('XA', 2), ('M', 2, 1), ('M', 0, 1), ('M', 1, 1), ('E', 4, 3), ('S', 7), ('E', 3, 3),
-    ('E', 6, 1), ('E', 5, 2), ('X1', 2, 1), ('X1', 0, 1), ('E', 4, 4), ('X1', 2, 0), ('M', 4, 0), ('E', 3, 4),
-    ('M', 4, 1), ('E', 7, 1), ('GY',), ('E', 6, 2), ('M', 3, 0), ('X2', 2, 1), ('M', 3, 1), ('E', 5, 3), ('X1', 4, 1),
-    ('X1', 4, 0), ('E', 7, 2), ('X1', 1, 1), ('E', 6, 3), ('E', 5, 4), ('X1', 3, 0), ('X1', 3, 1), ('GZ',),
-    ('X2', 0, 0), ('E', 7, 3), ('M', 5, 0), ('X2', 1, 0), ('E', 6, 4), ('X2', 0, 1), ('M', 5, 1), ('X2', 4, 0),
-    ('X2', 3, 0), ('X2', 4, 1), ('M', 6, 0), ('E', 7, 4), ('X2', 3, 1), ('M', 7, 0), ('X2', 2, 0), ('M', 7, 1),
-    ('X2', 1, 1), ('Y1', 4, 1), ('M', 6, 1), ('Y1', 0, 1), ('Y1', 1, 0), ('Y1', 3, 1), ('X1', 5, 1), ('Y1', 1, 1),
-    ('Y1', 4, 0), ('X1', 7, 1), ('X1', 6, 1), ('Y1', 2, 0), ('Y1', 2, 1), ('Y1', 0, 0), ('X1', 5, 0), ('Y1', 3, 0),
-    ('X1', 7, 0), ('X2', 5, 1), ('GA',), ('X2', 7, 1), ('X1', 6, 0), ('X2', 6, 1), ('X2', 5, 0), ('X2', 7, 0),
-    ('Y1', 7, 0), ('Y2', 1), ('Y2', 3), ('Y1', 5, 0), ('X2', 6, 0), ('Y1', 6, 1), ('Y1', 6, 0), ('Y1', 5, 1),
-    ('Y2', 4), ('Y2', 5), ('Y2', 0), ('Y2', 2), ('Y1', 7, 1), ('GO',), ('Y2', 7), ('Y2', 6),
+    ('S', 0), ('S', 1), ('XS',), ('S', 2), ('E', 0, 1), ('XO',), ('E', 1, 1), ('S', 3), ('E', 0, 2), ('GC',),
+    ('E', 2, 1), ('E', 1, 2), ('GS',), ('R', 0), ('E', 0, 3), ('R', 2), ('S', 4), ('E', 2, 2), ('R', 3), ('E', 1, 3),
+    ('S', 5), ('E', 3, 1), ('E', 0, 4), ('XA', 0), ('E', 2, 3), ('R', 1), ('XA', 2), ('E', 1, 4), ('E', 4, 1),
+    ('M', 0, 0), ('S', 6), ('GX',), ('M', 1, 0), ('I', 0, 0), ('I', 1, 0), ('E', 3, 2), ('E', 2, 4), ('X1', 0, 0),
+    ('E', 4, 2), ('S', 7), ('M', 2, 0), ('XA', 3), ('XA', 1), ('M', 1, 1), ('E', 6, 1), ('GY',), ('I', 1, 1),
+    ('M', 2, 1), ('M', 0, 1), ('X1', 1, 0), ('I', 2, 1), ('X2', 0, 0), ('E', 4, 3), ('E', 3, 3), ('X1', 2, 1),
+    ('X1', 1, 1), ('I', 0, 1), ('E', 5, 1), ('E', 6, 2), ('E', 4, 4), ('X1', 0, 1), ('I', 2, 0), ('X1', 2, 0),
+    ('E', 7, 1), ('E', 3, 4), ('M', 3, 0), ('E', 5, 2), ('M', 3, 1), ('M', 4, 0), ('X2', 2, 1), ('I', 4, 0),
+    ('E', 6, 3), ('E', 7, 2), ('I', 3, 0), ('X2', 1, 0), ('X2', 2, 0), ('M', 4, 1), ('X1', 3, 1), ('E', 5, 3),
+    ('I', 4, 1), ('E', 6, 4), ('X1', 3, 0), ('I', 3, 1), ('E', 7, 3), ('X1', 4, 0), ('X2', 1, 1), ('M', 6, 0),
+    ('E', 5, 4), ('M', 6, 1), ('X1', 4, 1), ('M', 5, 0), ('E', 7, 4), ('GZ',), ('X2', 3, 1), ('I', 5, 0), ('M', 5, 1),
+    ('X2', 0, 1), ('M', 7, 0), ('M', 7, 1), ('Y1', 2, 1), ('X2', 3, 0), ('I', 5, 1), ('Y1', 2, 0), ('Y1', 6, 1),
+    ('Y1', 6, 0), ('X2', 4, 1), ('X1', 5, 1), ('I', 7, 1), ('X1', 7, 1), ('Y1', 3, 1), ('X1', 5, 0), ('Y1', 0, 0),
+    ('GA',), ('Y1', 1, 1), ('I', 7, 0), ('X1', 7, 0), ('X2', 4, 0), ('X2', 5, 1), ('Y1', 3, 0), ('Y1', 1, 0),
+    ('Y1', 0, 1), ('X0', 6), ('X2', 7, 1), ('Y1', 4, 0), ('X2', 5, 0), ('Y1', 5, 0), ('Y2', 2), ('Y1', 5, 1),
+    ('Y2', 3), ('GO',), ('X2', 7, 0), ('Y2', 0), ('Y1', 4, 1), ('Y1', 7, 1), ('Y1', 7, 0), ('X1', 6, 0), ('Y2', 4),
+    ('Y2', 5), ('Y2', 1), ('Y2', 7), ('X2', 6, 0),
 )
 
 
@@ -54,6 +57,8 @@
     summed=pltpu.VMEM((8, 2, 128, 128), jnp.float32),
     yfar=pltpu.VMEM((8, 2, 64, 128), jnp.float32),
     ynear=pltpu.VMEM((8, 2, 128, 128), jnp.float32),
+    yfar4=pltpu.VMEM((max(1, len(YFIRST)), 2, 4, 64, 128), jnp.float32),
+    ynear4=pltpu.VMEM((max(1, len(YFIRST)), 2, 4, 128, 128), jnp.float32),
     nbuf=pltpu.VMEM((128, 8192), jnp.bfloat16),
     ngbuf=pltpu.VMEM((128, 8192), jnp.bfloat16),
     gain_c=pltpu.VMEM((2, 8, 8, 128), jnp.float32),
@@ -64,11 +69,11 @@
     gain_a=pltpu.VMEM((8, 8, 128), jnp.float32),
     load=pltpu.SemaphoreType.DMA((4,)),
     z_s=pltpu.SemaphoreType.DMA((8,)),
-    z_r=pltpu.SemaphoreType.DMA((8, 4)),
+    z_r=pltpu.SemaphoreType.DMA((8, 4, 2)),
     d_s=pltpu.SemaphoreType.DMA((8,)),
     d_r=pltpu.SemaphoreType.DMA((8,)),
     x1_s=pltpu.SemaphoreType.DMA,
-    x1_r=pltpu.SemaphoreType.DMA((4,)),
+    x1_r=pltpu.SemaphoreType.DMA((2, 4)),
     x2_s=pltpu.SemaphoreType.DMA,
     x2_r=pltpu.SemaphoreType.DMA((4,)),
     u_s=pltpu.SemaphoreType.DMA((8, 2)),
@@ -141,27 +146,13 @@
                 lanes = slice(64 * side, 64 * side + 64)
                 j = (pair * 2 + side) * 2 + low
                 b["gbuf"][j, z, core] = jnp.concatenate([block[:, lanes] for block in blocks], axis=1)
-    load_x.wait()
-    for k in range(8):
-        b["xt"][0, :, k * 256 : (k + 1) * 256] = b["xown"][k * 256 : (k + 1) * 256, :].T
-    load_n.wait()
-    load_ng.wait()
-
-    def block_sum(i, carry):
-        for k in range(8):
-            lanes = pl.ds(pl.multiple_of(i * 1024 + k * 128, 128), 128)
-            terms = b["nbuf"][:, lanes].astype(jnp.float32) * b["ngbuf"][:, lanes].astype(jnp.float32)
-            b["gain_c"][core, i, k : k + 1, :] = jnp.sum(terms, axis=0, keepdims=True)
-        return carry
-
-    lax.fori_loop(0, 8, block_sum, 0)
     pl.semaphore_wait(barrier, len(greeted))
 
     def z_send(j, d, s):
         piece = b["gbuf"].at[j, ring(z - (s - 1) * both[d], 8), core]
         if s == 4:
             piece = piece.at[pl.ds(64 * d, 64)]
-        start(piece, piece, b["z_s"].at[j], b["z_r"].at[j, s - 1], at_z(both[d]))
+        start(piece, piece, b["z_s"].at[j], b["z_r"].at[j, s - 1, d], at_z(both[d]))
 
     def d_send(j, d, s):
         piece = b["gbuf"].at[j, ring(z - s * both[d], 8), core]
@@ -169,21 +160,27 @@
             piece = piece.at[pl.ds(64 * d, 64)]
         start(piece, piece, b["d_s"].at[j], b["d_r"].at[j], sibling)
 
+    def XO():
+        load_x.wait()
+        for k in range(8):
+            b["xt"][0, :, k * 256 : (k + 1) * 256] = b["xown"][k * 256 : (k + 1) * 256, :].T
+
     def S(j):
         for d in range(2):
             z_send(j, d, 1)
         d_send(j, 0, 0)
 
     def E(j, s):
-        landed(b["gbuf"].at[j, pl.ds(0, 2 if s < 4 else 1), core], b["z_r"].at[j, s - 1])
         for d in range(2):
+            piece = b["gbuf"].at[j, 0, core]
+            landed(piece if s < 4 else piece.at[pl.ds(0, 64)], b["z_r"].at[j, s - 1, d])
             if s < 4:
                 z_send(j, d, s + 1)
             d_send(j, d, s)
 
     def relay_copy(d, m):
         rows = pl.multiple_of(away_rows + d * 1024 + m * 256, 256)
-        return x_hbm.at[pl.ds(rows, 256), :], b["relay"].at[d, m], b["x1_s"], b["x1_r"].at[m], at_y(both[d])
+        return x_hbm.at[pl.ds(rows, 256), :], b["relay"].at[d, m], b["x1_s"], b["x1_r"].at[d, m], at_y(both[d])
 
     def onward_copy(d, m):
         return b["relay"].at[d, m], b["xoth"].at[d, m], b["x2_s"], b["x2_r"].at[m], at_y(both[d])
@@ -194,8 +191,8 @@
                 start(*relay_copy(d, m))
 
     def R(m):
-        landed(b["relay"].at[:, m], b["x1_r"].at[m])
         for d in range(2):
+            landed(b["relay"].at[d, m], b["x1_r"].at[d, m])
             start(*onward_copy(d, m))
 
     def XA(m):
@@ -211,6 +208,19 @@
 
     def arrived(count, buf, sem):
         landed(buf.at[pl.ds(0, count - 1)], b["g_r"].at[sem])
+
+    def GC():
+        load_n.wait()
+        load_ng.wait()
+
+        def block_sum(i, carry):
+            for k in range(8):
+                lanes = pl.ds(pl.multiple_of(i * 1024 + k * 128, 128), 128)
+                terms = b["nbuf"][:, lanes].astype(jnp.float32) * b["ngbuf"][:, lanes].astype(jnp.float32)
+                b["gain_c"][core, i, k : k + 1, :] = jnp.sum(terms, axis=0, keepdims=True)
+            return carry
+
+        lax.fori_loop(0, 8, block_sum, 0)
 
     def GS():
         mine = b["gain_c"].at[core]
@@ -264,10 +274,23 @@
                 packed.append(jnp.where(low, pltpu.roll(upper, 64, 1), lower))
         for k in range(4):
             b["part"][j, o, k] = packed[k] + packed[4 + k]
-        far = ring(x + 2, 4)
+        if j in YFIRST:
+            y_first_sends(j, o)
+        else:
+            far_sends(j, o)
+
+    def far_sends(j, o):
         for d in range(2):
             half = pl.ds(64 * d, 64)
-            start(b["part"].at[j, o, far, half], b["xfar"].at[j, o, d], b["u_s"].at[j, o], b["far_r"].at[j, o], at_x(both[d]))
+            start(
+                b["part"].at[j, o, ring(x + 2, 4), half],
+                b["xfar"].at[j, o, d],
+                b["u_s"].at[j, o],
+                b["far_r"].at[j, o],
+                at_x(both[d]),
+            )
+
+    def I(j, o):
         for d in range(2):
             near_send(j, o, d, 1 - d)
 
@@ -281,13 +304,18 @@
             at_x(both[d]),
         )
 
+    def where_owned(j):
+        return pl.when(ylo == j % 2) if j in YFIRST else lambda step: step()
+
     def X1(j, o):
-        landed(b["xfar"].at[j, o], b["far_r"].at[j, o])
-        for d in range(2):
-            there = ring(x + both[d], 4)
-            rows = pl.ds(64 * d, 64)
-            b["part"][j, o, there, rows] = b["part"][j, o, there, rows] + b["xfar"][j, o, d]
-            near_send(j, o, d, d)
+        @where_owned(j)
+        def _():
+            landed(b["xfar"].at[j, o], b["far_r"].at[j, o])
+            for d in range(2):
+                there = ring(x + both[d], 4)
+                rows = pl.ds(64 * d, 64)
+                b["part"][j, o, there, rows] = b["part"][j, o, there, rows] + b["xfar"][j, o, d]
+                near_send(j, o, d, d)
 
     def role(j, o):
         owns = ylo == j % 2
@@ -316,7 +344,21 @@
             y_target(ahead),
         )
 
+    def put(j, total):
+        total = total * 0.125
+        lanes = slice((j // 2) * 64, (j // 2) * 64 + 64)
+        out_ref[:128, lanes] = total[:, :64]
+        out_ref[128:, lanes] = total[:, 64:]
+
     def X2(j, o):
+        if j in YFIRST:
+
+            @where_owned(j)
+            def _():
+                landed(b["xnear"].at[j, o], b["near_r"].at[j, o])
+                put(j, b["part"][j, o, x] + (b["xnear"][j, o, 0] + b["xnear"][j, o, 1]))
+
+            return
         landed(b["xnear"].at[j, o], b["near_r"].at[j, o])
         b["summed"][j, o] = b["part"][j, o, x] + (b["xnear"][j, o, 0] + b["xnear"][j, o, 1])
         owns, ahead = role(j, o)
@@ -331,11 +373,55 @@
         def _():
             copy(*y_near(j, o, ahead, False)).start()
 
+    def y4_far(j, o, d):
+        rows, slot = pl.ds(64 * d, 64), YFIRST.index(j)
+        return b["part"].at[j, o, :, rows], b["yfar4"].at[slot, feature(o)], b["y_s"].at[j, o], b["yf_r"].at[j, feature(o)], at_y(both[d])
+
+    def y4_near(j, o, ahead, late):
+        half = ahead if late else 1 - ahead
+        rows = pl.ds(pl.multiple_of(64 * half, 64), 64)
+        return (
+            b["part"].at[j, o, :, rows],
+            b["ynear4"].at[YFIRST.index(j), ahead, :, rows],
+            b["y_s"].at[j, o],
+            b["yn_r"].at[j],
+            y_target(ahead),
+        )
+
+    def y_first_sends(j, o):
+        owns, ahead = role(j, o)
+        if o == 1:
+
+            @pl.when(owns)
+            def _():
+                for d in range(2):
+                    start(*y4_far(j, o, d))
+
+        @pl.when(jnp.logical_not(owns))
+        def _():
+            start(*y4_near(j, o, ahead, False))
+
+    def X0(j):
+        @where_owned(j)
+        def _():
+            slot = YFIRST.index(j)
+            landed(b["ynear4"].at[slot], b["yn_r"].at[j])
+            b["part"][j, 0] = b["part"][j, 0] + (b["ynear4"][slot, 0] + b["ynear4"][slot, 1])
+            far_sends(j, 0)
+            I(j, 0)
+
     def Y1(j, o):
         owns, ahead = role(j, o)
 
         @pl.when(jnp.logical_not(owns))
         def _():
+            if j in YFIRST:
+                slot = YFIRST.index(j)
+                landed(b["yfar4"].at[slot, feature(o)], b["yf_r"].at[j, feature(o)])
+                rows = pl.ds(pl.multiple_of(64 * ahead, 64), 64)
+                b["part"][j, o, :, rows] = b["part"][j, o, :, rows] + b["yfar4"][slot, feature(o)]
+                start(*y4_near(j, o, ahead, True))
+                return
             landed(b["yfar"].at[j, feature(o)], b["yf_r"].at[j, feature(o)])
             rows = pl.ds(pl.multiple_of(64 * ahead, 64), 64)
             b["summed"][j, o, rows] = b["summed"][j, o, rows] + b["yfar"][j, feature(o)]
@@ -347,13 +433,9 @@
         @pl.when(owns)
         def _():
             landed(b["ynear"].at[j], b["yn_r"].at[j])
-            total = b["summed"][j, 0] + (b["ynear"][j, 0] + b["ynear"][j, 1])
-            total = total * 0.125
-            lanes = slice((j // 2) * 64, (j // 2) * 64 + 64)
-            out_ref[:128, lanes] = total[:, :64]
-            out_ref[128:, lanes] = total[:, 64:]
-
-    steps = dict(S=S, E=E, XS=XS, R=R, XA=XA, GS=GS, GX=GX, GY=GY, GZ=GZ, GA=GA, GO=GO, M=M, X1=X1, X2=X2, Y1=Y1, Y2=Y2)
+            put(j, b["summed"][j, 0] + (b["ynear"][j, 0] + b["ynear"][j, 1]))
+
+    steps = dict(XO=XO, GC=GC, I=I, X0=X0, S=S, E=E, XS=XS, R=R, XA=XA, GS=GS, GX=GX, GY=GY, GZ=GZ, GA=GA, GO=GO, M=M, X1=X1, X2=X2, Y1=Y1, Y2=Y2)
     for name, *which in ORDER:
         steps[name](*which)
 
@@ -367,15 +449,23 @@
         landed(b["gbuf"].at[j, pl.ds(0, 7), 0], b["z_s"].at[j])
         landed(b["gbuf"].at[j, :, 0], b["d_s"].at[j])
         for o in range(2):
-            landed(b["part"].at[j, o, pl.ds(0, 3)], b["u_s"].at[j, o])
+            if j not in YFIRST:
+                landed(b["part"].at[j, o, pl.ds(0, 3)], b["u_s"].at[j, o])
+            y_sent = b["part"].at[j, o] if j in YFIRST else b["summed"].at[j, o]
+            if o == 1:
+                landed(y_sent, b["y_s"].at[j, o])
+                continue
             owns, _ = role(j, o)
-            if o == 1:
-                landed(b["summed"].at[j, o], b["y_s"].at[j, o])
-            else:
-
-                @pl.when(jnp.logical_not(owns))
+
+            @pl.when(jnp.logical_not(owns))
+            def _():
+                landed(y_sent, b["y_s"].at[j, o])
+
+            if j in YFIRST:
+
+                @pl.when(owns)
                 def _():
-                    landed(b["summed"].at[j, o], b["y_s"].at[j, o])
+                    landed(b["part"].at[j, o, pl.ds(0, 3)], b["u_s"].at[j, o])
 
 
 def finish(grad_ref, gain_ref, first_ref, second_ref, new_first_ref, new_second_ref, update_ref, gain_grad_ref):

time: 80 us -> 75.9 us (0.949); the launches traced: 79.9 us -> 74.9 us
  Pallas kernels: 79.3 us -> 74.3 us
    pallas_call x1, Pallas kernels: 77.2 us -> 72.2 us  [shards(): pl.pallas_call(exchange, out_shape=(jax.ShapeDtypeStruct((256, 256), jnp....]
where the time goes in v3:
time: 75.9 us; the launch traced here: 74.9 us
  Pallas kernels  74.3 us (98%)
    pallas_call x1, Pallas kernels, shards(): pl.pallas_call(exchange, out_shape=(jax.ShapeDtypeStruct((256, 256), jnp....  72.2 us
    pallas_call x1, Pallas kernels, shards(): pl.pallas_call(finish, out_shape=(block, block, block, jax.ShapeDtypeStru...  2.11 us

profile of v3, /device:TPU:1, one launch (start us, length us, event | category | flops | bytes accessed | tf_op | source)
XLA Modules:
  0.0 74.9 jit_solution(11793850582850804456)
XLA Ops:
  0.6 72.2 %exchange.1 = (f32[256,256]{1,0:T(8,128)}, f32[8,8,128]{2,1,0:T(8,128)}) custom-call(bf16[4096,256]{1,0:T(8,128)(2,1)} %bitcast.9, bf16[128,2048]{1,0:T(8,128)(2,1)} %bitcast.12, bf16[128,8192]{1,0:T(8,128)(2,1)} %bitcast.10, bf16[128,8192]{1,0:T(8,128)(2,1)} %bitcast.11), custom_call_target="tpu_custom_call" | custom-call | tf_op jit(solution)/shard_map/exchange/pallas_call | solution.py:486
  72.8 2.1 %finish.1 = (f32[256,256]{1,0:T(8,128)}, f32[256,256]{1,0:T(8,128)}, f32[256,256]{1,0:T(8,128)}, f32[1,8192]{1,0:T(1,128)}) custom-call(f32[256,256]{1,0:T(8,128)} %get-tuple-element.10.grad_ref, f32[8,8,128]{2,1,0:T(8,128)} %get-tuple-element.11.gain_ref, f32[256,256]{1,0:T(8,128)} %bitcast.13, f32[256,256]{1,0:T(8,128)} %bitcast.14), custom_call_target="tpu_custom_call" | custom-call | tf_op jit(solution)/shard_map/finish/pallas_call | solution.py:498
